TPU v7x, 32 devices: a whole 2x2x4 slice. The times are simulated.
32 devices in a mesh: sy: 4 (over y, x), sx: 4 (over z), wl: 2 (over core).
Axes of the slice: x: 2, y: 2, z: 4, core: 2. Of those that a mesh axis runs over, the one named last changes fastest.
Arguments:
- interface_map: bfloat16 [8, 4, 1536, 2, 1536], P(('wl', 'sy'), 'sx'), parts along dimension 0, may hold values from -0.0625 to 0.0625
- source_trace: float32 [8, 4, 2, 64, 4, 384], P(('wl', 'sy'), 'sx'), parts along dimension 0, may hold values from -6 to 6
- restriction: float32 [8, 4, 2, 32, 4, 384], P(('wl', 'sy'), 'sx'), parts along dimension 0, may hold values from -0.02734375 to 0.02734375
- prolongation: float32 [8, 4, 2, 32, 4, 384], P(('wl', 'sy'), 'sx'), parts along dimension 0, may hold values from -0.109375 to 0.109375
- coarse_inverse: float32 [4, 32, 32], P('wl'), parts along dimension 0, may hold values from -0.75 to 0.75
Outputs:
- traces: float32 [8, 4, 2, 64, 4, 384], P(('wl', 'sy'), 'sx'), parts along dimension 0
- coarse_coef: float32 [4, 64, 32], P('wl'), parts along dimension 0
There are 2 independent parts, one for each index of `wl`. A program takes and returns all parts, laid end to end along the dimension named above; each array names one. Nothing has to cross between parts.
All inputs are finite; a program needn't handle non-finite values.
Results may differ from a plain program's by a relative error of at most 0.0025.
Values sent between devices are 32-bit elements; how exact they have to be, the bound alone decides.
A program may use at most 128 MiB of HBM per device.

v0:
```python
import jax
import jax.numpy as jnp
from jax import lax
from jax.sharding import PartitionSpec as P

ITERS = 6
PRECISE = lax.Precision.HIGHEST


def shifted(value, axis, by):
    peers = lax.axis_size(axis)
    pairs = [(i, i + by) for i in range(peers) if 0 <= i + by < peers]
    return lax.ppermute(value, axis, pairs)


def with_halo(value, sides, width):
    for axis, dim in sides:
        peers, length = (lax.axis_size(axis), value.shape[dim])
        up = [(i, (i + 1) % peers) for i in range(peers - 1)]
        down = [(j, i) for i, j in up]
        last = lax.slice_in_dim(value, length - width, length, axis=dim)
        initial = lax.slice_in_dim(value, 0, width, axis=dim)
        before = lax.ppermute(last, axis, up)
        after = lax.ppermute(initial, axis, down)
        value = jnp.concatenate([before, value, after], axis=dim)
    return value


def complex_pair(left_real, left_imag, right_real, right_imag, pattern):
    real_part = jnp.einsum(pattern, left_real, right_real, precision=PRECISE) - jnp.einsum(
        pattern, left_imag, right_imag, precision=PRECISE
    )
    imag_part = jnp.einsum(pattern, left_real, right_imag, precision=PRECISE) + jnp.einsum(
        pattern, left_imag, right_real, precision=PRECISE
    )
    return jnp.stack([real_part, imag_part])


def corner_values(outgoing):
    corner_northwest = outgoing[..., 0, 0] + outgoing[..., 2, 0]
    corner_northeast = outgoing[..., 0, -1] + outgoing[..., 3, 0]
    corner_southwest = outgoing[..., 1, 0] + outgoing[..., 2, -1]
    corner_southeast = outgoing[..., 1, -1] + outgoing[..., 3, -1]
    return (corner_northwest, corner_northeast, corner_southwest, corner_southeast)


def assemble(
    from_north,
    from_south,
    from_west,
    from_east,
    into_northwest,
    into_northeast,
    into_southwest,
    into_southeast,
):
    north_side = (
        from_north.at[..., 0].add(0.5 * into_northwest).at[..., -1].add(0.5 * into_northeast)
    )
    south_side = (
        from_south.at[..., 0].add(0.5 * into_southwest).at[..., -1].add(0.5 * into_southeast)
    )
    west_side = from_west.at[..., 0].add(0.5 * into_northwest).at[..., -1].add(0.5 * into_southwest)
    east_side = from_east.at[..., 0].add(0.5 * into_northeast).at[..., -1].add(0.5 * into_southeast)
    return jnp.stack([north_side, south_side, west_side, east_side], axis=-2)


def restrict_sum(traces, weights):
    src_count, side_len = (traces.shape[1], traces.shape[3])
    coarse_width = weights.shape[1]
    flat_traces = traces.reshape(2, src_count, 4 * side_len)
    flat_weights = weights.reshape(2, coarse_width, 4 * side_len)
    return complex_pair(
        flat_traces[0], flat_traces[1], flat_weights[0], flat_weights[1], "sk,nk->sn"
    )


def outgoing_traces(traces, map_shard, source_shard):
    src_count, side_len = (traces.shape[1], traces.shape[3])
    row_block = traces.astype(jnp.bfloat16).reshape(2 * src_count, 4 * side_len)
    map_table = map_shard.reshape(4 * side_len, 8 * side_len)
    product = jnp.dot(row_block, map_table, preferred_element_type=jnp.float32).reshape(
        2, src_count, 2, 4 * side_len
    )
    real_part = product[0, :, 0] - product[1, :, 1]
    imag_part = product[0, :, 1] + product[1, :, 0]
    return jnp.stack([real_part, imag_part]).reshape(2, src_count, 4, side_len) + source_shard


def exchange_direct(outgoing):
    from_north = shifted(outgoing[:, :, 1], "sy", 1)
    from_south = shifted(outgoing[:, :, 0], "sy", -1)
    from_west = shifted(outgoing[:, :, 3], "sx", 1)
    from_east = shifted(outgoing[:, :, 2], "sx", -1)
    corner_northwest, corner_northeast, corner_southwest, corner_southeast = corner_values(outgoing)
    corner_grid = jnp.stack(
        [
            jnp.stack([corner_northwest, corner_northeast]),
            jnp.stack([corner_southwest, corner_southeast]),
        ]
    )
    padded = with_halo(corner_grid, (("sy", 0), ("sx", 1)), 1)
    return assemble(
        from_north,
        from_south,
        from_west,
        from_east,
        padded[0, 0],
        padded[0, 3],
        padded[3, 0],
        padded[3, 3],
    )


def sender_restriction(weights):
    receive_northwest = 0.5 * (weights[:, :, 0, 0] + weights[:, :, 2, 0])
    receive_northeast = 0.5 * (weights[:, :, 0, -1] + weights[:, :, 3, 0])
    receive_southwest = 0.5 * (weights[:, :, 1, 0] + weights[:, :, 2, -1])
    receive_southeast = 0.5 * (weights[:, :, 1, -1] + weights[:, :, 3, -1])
    empty_slot = jnp.zeros_like(weights[:, :, 0])

    def spread_slot(vector):
        return jnp.broadcast_to(vector[:, :, None], empty_slot.shape)

    weight_grid = jnp.stack(
        [
            jnp.stack(
                [spread_slot(receive_northwest), weights[:, :, 0], spread_slot(receive_northeast)]
            ),
            jnp.stack([weights[:, :, 2], empty_slot, weights[:, :, 3]]),
            jnp.stack(
                [spread_slot(receive_southwest), weights[:, :, 1], spread_slot(receive_southeast)]
            ),
        ]
    )
    padded = with_halo(weight_grid, (("sy", 0), ("sx", 1)), 1)
    weight_northwest = padded[0, 0][..., 0]
    weight_northeast = padded[0, 4][..., 0]
    weight_southwest = padded[4, 0][..., 0]
    weight_southeast = padded[4, 4][..., 0]
    north_weights = padded[0, 2].at[..., 0].add(weight_northwest).at[..., -1].add(weight_northeast)
    south_weights = padded[4, 2].at[..., 0].add(weight_southwest).at[..., -1].add(weight_southeast)
    west_weights = padded[2, 0].at[..., 0].add(weight_northwest).at[..., -1].add(weight_southwest)
    east_weights = padded[2, 4].at[..., 0].add(weight_northeast).at[..., -1].add(weight_southeast)
    return jnp.stack([north_weights, south_weights, west_weights, east_weights], axis=2)


def per_device(interface_map, source_trace, restriction, prolongation, coarse_inverse):
    source_shard = source_trace[0, 0]
    weights = restriction[0, 0]
    src_count, side_len = (source_shard.shape[1], source_shard.shape[3])
    coarse_width = weights.shape[1]
    lift_flat = prolongation[0, 0].reshape(2, coarse_width, 4 * side_len)
    traces = jnp.zeros(source_shard.shape, jnp.float32)
    coef_now = jnp.zeros((2, src_count, coarse_width), jnp.float32)
    coarse_total = coef_now
    sender_weights = sender_restriction(weights)
    for sweep_index in range(ITERS):
        coef_now = complex_pair(
            coarse_total[0], coarse_total[1], coarse_inverse[0], coarse_inverse[1], "sn,nq->sq"
        )
        spread = complex_pair(coef_now[0], coef_now[1], lift_flat[0], lift_flat[1], "sn,nk->sk")
        corrected = traces + spread.reshape(traces.shape)
        outgoing = outgoing_traces(corrected, interface_map, source_shard)
        if sweep_index + 1 < ITERS:
            coarse_total = lax.psum(restrict_sum(outgoing, sender_weights), ("sy", "sx"))
        traces = exchange_direct(outgoing)
    return (traces[None, None], coef_now)


def solution(mesh):
    return jax.shard_map(
        per_device,
        mesh=mesh,
        in_specs=(
            P(("wl", "sy"), "sx", None, None, None),
            P(("wl", "sy"), "sx", None, None, None, None),
            P(("wl", "sy"), "sx", None, None, None, None),
            P(("wl", "sy"), "sx", None, None, None, None),
            P("wl", None, None),
        ),
        out_specs=(P(("wl", "sy"), "sx", None, None, None, None), P("wl", None, None)),
        check_vma=False,
    )
```

profile of v0, /device:TPU:20, one launch (start us, length us, event | category | flops | bytes accessed | tf_op | source)
XLA Modules:
  0.0 721.0 jit_solution(16520153187485234129)
XLA Ops:
  2.5 9.8 %copy.272 = bf16[192,8,2,1536]{3,1,2,0:T(8,128)(2,1)} copy(bf16[192,8,2,1536]{3,2,1,0:T(2,128)(2,1)} %bitcast.751) | data formatting | bytes 18874368
  12.3 12.7 %copy.114 = bf16[3072,1536]{1,0:T(8,128)(2,1)} copy(bf16[3072,1536]{0,1:T(8,128)(2,1)} %bitcast.726) | data formatting | bytes 18874368 | tf_op jit(solution)/shard_map/dot_general | solution.py:82
  27.2 6.8 fusion.29
  36.2 2.3 collective-permute-start.7
  38.8 3.4 collective-permute-start.2
  42.2 2.5 collective-permute-start.1
  44.7 1.9 collective-permute-start
  46.6 3.5 collective-permute-start.6
  51.9 4.8 collective-permute-start.5
  56.8 2.3 collective-permute-start.4
  60.1 2.2 collective-permute-done.4
  64.9 2.8 collective-permute-done.3
  71.3 4.8 collective-permute-start.9
  96.7 3.9 collective-permute-start.11
  102.5 5.2 collective-permute-done.11
  113.1 70.4 %psum.35 = f32[2,64,32]{1,2,0:T(8,128)S(1)} all-reduce(f32[2,64,32]{1,2,0:T(8,128)S(1)} %pad_maximum_fusion.1), channel_id=1, replica_groups=mesh['sy'=4,'sx'=4,'wl'=2] {'sy','sx'}, use_global_device_ids=true, to_apply=%region_0.0 | all-reduce | flops 4096 | bytes 32768 | tf_op jit(solution)/shard_map/psum | solution.py:166
  188.5 6.8 fusion.40
  198.8 72.4 %psum.36 = f32[2,64,32]{1,2,0:T(8,128)S(1)} all-reduce(f32[2,64,32]{1,2,0:T(8,128)S(1)} %pad_maximum_fusion.2), channel_id=1, replica_groups=mesh['sy'=4,'sx'=4,'wl'=2] {'sy','sx'}, use_global_device_ids=true, to_apply=%region_1.0 | all-reduce | flops 4096 | bytes 32768 | tf_op jit(solution)/shard_map/psum | solution.py:166
  271.7 1.9 collective-permute-start.14
  273.6 3.9 collective-permute-start.13
  279.5 3.7 collective-permute-start.19
  283.2 1.9 collective-permute-start.12
  285.2 2.2 collective-permute-start.18
  287.4 4.8 collective-permute-start.17
  292.2 5.5 collective-permute-start.16
  301.1 3.7 collective-permute-done.15
  313.6 6.8 fusion.38
  323.9 70.6 %psum.37 = f32[2,64,32]{1,2,0:T(8,128)S(1)} all-reduce(f32[2,64,32]{1,2,0:T(8,128)S(1)} %pad_maximum_fusion.3), channel_id=1, replica_groups=mesh['sy'=4,'sx'=4,'wl'=2] {'sy','sx'}, use_global_device_ids=true, to_apply=%region_2.0 | all-reduce | flops 4096 | bytes 32768 | tf_op jit(solution)/shard_map/psum | solution.py:166
  394.9 1.9 collective-permute-start.22
  396.9 3.9 collective-permute-start.21
  404.8 1.9 collective-permute-start.20
  406.7 3.9 collective-permute-start.26
  410.6 4.8 collective-permute-start.25
  415.5 5.6 collective-permute-start.24
  424.4 3.7 collective-permute-done.23
  433.6 2.1 scatter-add.229
  437.1 6.8 fusion.36
  447.4 70.6 %psum.38 = f32[2,64,32]{1,2,0:T(8,128)S(1)} all-reduce(f32[2,64,32]{1,2,0:T(8,128)S(1)} %pad_maximum_fusion.4), channel_id=1, replica_groups=mesh['sy'=4,'sx'=4,'wl'=2] {'sy','sx'}, use_global_device_ids=true, to_apply=%region_3.0 | all-reduce | flops 4096 | bytes 32768 | tf_op jit(solution)/shard_map/psum | solution.py:166
  518.4 1.9 collective-permute-start.30
  520.3 3.9 collective-permute-start.29
  528.2 1.9 collective-permute-start.28
  530.1 3.9 collective-permute-start.34
  534.1 4.8 collective-permute-start.33
  539.0 5.5 collective-permute-start.32
  547.9 3.7 collective-permute-done.31
  560.3 6.8 fusion.34
  570.5 70.8 %psum.39 = f32[2,64,32]{1,2,0:T(8,128)S(1)} all-reduce(f32[2,64,32]{1,2,0:T(8,128)S(1)} %pad_maximum_fusion.5), channel_id=1, replica_groups=mesh['sy'=4,'sx'=4,'wl'=2] {'sy','sx'}, use_global_device_ids=true, to_apply=%region_4.0 | all-reduce | flops 4096 | bytes 32768 | tf_op jit(solution)/shard_map/psum | solution.py:166
  641.7 1.9 collective-permute-start.38
  643.7 3.9 collective-permute-start.37
  649.6 1.9 collective-permute-start.43
  653.5 3.9 collective-permute-start.42
  657.4 4.8 collective-permute-start.41
  662.3 5.5 collective-permute-start.40
  671.2 3.7 collective-permute-done.39
  678.2 6.8 fusion.32
  685.9 1.9 collective-permute-start.46
  687.8 3.9 collective-permute-start.45
  694.2 4.2 collective-permute-start.48
  698.4 1.9 collective-permute-start.51
  700.4 3.0 collective-permute-start.44
  703.4 3.9 collective-permute-start.50
  707.3 3.7 collective-permute-start.49
  711.1 1.9 collective-permute-start.47
  713.1 3.5 collective-permute-done.47
  (390 shorter events, 124.8 us)
Async XLA Ops:
  12.3 12.7 %copy-start.2 = (f32[1,1,2,32,4,384]{5,4,3,2,1,0:T(4,128)S(1)}, f32[1,1,2,32,4,384]{5,4,3,2,1,0:T(4,128)}, u32[]{:S(2)}) copy-start(f32[1,1,2,32,4,384]{5,4,3,2,1,0:T(4,128)} %param.120) | copy-start | bytes 1179652
  34.1 1.1 copy-start
  35.3 14.8 %copy-start.3 = (f32[1,1,2,32,4,384]{5,4,3,2,1,0:T(4,128)S(1)}, f32[1,1,2,32,4,384]{5,4,3,2,1,0:T(4,128)}, u32[]{:S(2)}) copy-start(f32[1,1,2,32,4,384]{5,4,3,2,1,0:T(4,128)} %param.119) | copy-start | bytes 1179652
  36.2 43.0 %collective-permute-start.7 = (f32[2,64,384]{2,1,0:T(8,128)}, f32[2,64,384]{2,1,0:T(8,128)S(1)}, u32[]{:S(2)}, u32[]{:S(2)}) collective-permute-start(f32[2,64,384]{2,1,0:T(8,128)} %get-tuple-element.741), channel_id=1, source_target_pairs={{2,0},{4,2},{6,4},{3,1},{5,3},{7,5},{10,8},{12,10},{14,12},{11,9},... | collective-permute-start | bytes 589832 | tf_op jit(solution)/shard_map/ppermute | solution.py:13
  38.8 13.1 %collective-permute-start.2 = (f32[1,2,2,64]{3,2,1,0:T(2,128)S(1)}, f32[1,2,2,64]{3,2,1,0:T(2,128)S(1)}, u32[]{:S(2)}, u32[]{:S(2)}) collective-permute-start(f32[1,2,2,64]{3,2,1,0:T(2,128)S(1)} %maximum_bitcast_fusion.7), channel_id=1, source_target_pairs={{8,0},{16,8},{24,16},{9,1},{17,9},{25,17},{10,2},{18,10},{26,18},{... | collective-permute-start | bytes 3080 | tf_op jit(solution)/shard_map/ppermute | solution.py:24
  42.2 14.5 %collective-permute-start.1 = (f32[1,2,2,64]{3,2,1,0:T(2,128)S(1)}, f32[1,2,2,64]{3,2,1,0:T(2,128)S(1)}, u32[]{:S(2)}, u32[]{:S(2)}) collective-permute-start(f32[1,2,2,64]{3,2,1,0:T(2,128)S(1)} %maximum_bitcast_fusion.6), channel_id=1, source_target_pairs={{0,8},{8,16},{16,24},{1,9},{9,17},{17,25},{2,10},{10,18},{18,26},{... | collective-permute-start | bytes 3080 | tf_op jit(solution)/shard_map/ppermute | solution.py:23
  44.7 26.6 %collective-permute-start = (f32[2,64,384]{2,1,0:T(8,128)S(1)}, f32[2,64,384]{2,1,0:T(8,128)}, u32[]{:S(2)}, u32[]{:S(2)}) collective-permute-start(f32[2,64,384]{2,1,0:T(8,128)S(1)} %get-tuple-element.740), channel_id=1, source_target_pairs={{0,8},{8,16},{16,24},{1,9},{9,17},{17,25},{2,10},{10,18},{18,26},{... | collective-permute-start | bytes 589832 | tf_op jit(solution)/shard_map/ppermute | solution.py:13
  46.6 29.5 %collective-permute-start.6 = (f32[2,64,384]{2,1,0:T(8,128)}, f32[2,64,384]{2,1,0:T(8,128)}, u32[]{:S(2)}, u32[]{:S(2)}) collective-permute-start(f32[2,64,384]{2,1,0:T(8,128)} %get-tuple-element.743), channel_id=1, source_target_pairs={{0,2},{2,4},{4,6},{1,3},{3,5},{5,7},{8,10},{10,12},{12,14},{9,11},... | collective-permute-start | bytes 589832 | tf_op jit(solution)/shard_map/ppermute | solution.py:13
  51.9 31.4 %collective-permute-start.5 = (f32[2,64,384]{2,1,0:T(8,128)}, f32[2,64,384]{2,1,0:T(8,128)}, u32[]{:S(2)}, u32[]{:S(2)}) collective-permute-start(f32[2,64,384]{2,1,0:T(8,128)} %get-tuple-element.742), channel_id=1, source_target_pairs={{8,0},{16,8},{24,16},{9,1},{17,9},{25,17},{10,2},{18,10},{26,18},{... | collective-permute-start | bytes 589832 | tf_op jit(solution)/shard_map/ppermute | solution.py:13
  56.8 5.5 collective-permute-start.4
  62.3 5.5 collective-permute-start.3
  67.8 18.6 %collective-permute-start.8 = (f32[1,3,2,32,384]{4,3,2,1,0:T(8,128)}, f32[1,3,2,32,384]{4,3,2,1,0:T(8,128)S(1)}, u32[]{:S(2)}, u32[]{:S(2)}) collective-permute-start(f32[1,3,2,32,384]{4,3,2,1,0:T(8,128)} %maximum_bitcast_fusion.3), channel_id=1, source_target_pairs={{0,8},{8,16},{16,24},{1,9},{9,17},{17,25},{2,10},{10,18},{18,26},{... | collective-permute-start | bytes 884744 | tf_op jit(solution)/shard_map/ppermute | solution.py:23
  71.3 16.2 %collective-permute-start.9 = (f32[1,3,2,32,384]{4,3,2,1,0:T(8,128)}, f32[1,3,2,32,384]{4,3,2,1,0:T(8,128)S(1)}, u32[]{:S(2)}, u32[]{:S(2)}) collective-permute-start(f32[1,3,2,32,384]{4,3,2,1,0:T(8,128)} %maximum_bitcast_fusion.4), channel_id=1, source_target_pairs={{8,0},{16,8},{24,16},{9,1},{17,9},{25,17},{10,2},{18,10},{26,18},{... | collective-permute-start | bytes 884744 | tf_op jit(solution)/shard_map/ppermute | solution.py:24
  87.5 4.3 copy-start.5
  87.5 7.6 %copy-start.4 = (f32[2,64,1,1]{3,1,0,2:T(8,128)S(1)}, f32[2,64,1,1]{3,1,0,2:T(8,128)}, u32[]{:S(2)}) copy-start(f32[2,64,1,1]{3,1,0,2:T(8,128)} %get-tuple-element.804) | copy-start | bytes 1540
  88.5 12.1 %collective-permute-start.10 = (f32[5,1,2,32,384]{4,3,2,1,0:T(8,128)}, f32[5,1,2,32,384]{4,3,2,1,0:T(8,128)}, u32[]{:S(2)}, u32[]{:S(2)}) collective-permute-start(f32[5,1,2,32,384]{4,3,2,1,0:T(8,128)} %get-tuple-element.718), channel_id=1, source_target_pairs={{0,2},{2,4},{4,6},{1,3},{3,5},{5,7},{8,10},{10,12},{12,14},{9,11},... | collective-permute-start | bytes 1474568 | tf_op jit(solution)/shard_map/ppermute | solution.py:23
  96.7 11.0 %collective-permute-start.11 = (f32[5,1,2,32,384]{4,3,2,1,0:T(8,128)}, f32[5,1,2,32,384]{4,3,2,1,0:T(8,128)}, u32[]{:S(2)}, u32[]{:S(2)}) collective-permute-start(f32[5,1,2,32,384]{4,3,2,1,0:T(8,128)} %get-tuple-element.719), channel_id=1, source_target_pairs={{2,0},{4,2},{6,4},{3,1},{5,3},{7,5},{10,8},{12,10},{14,12},{11,9},... | collective-permute-start | bytes 1474568 | tf_op jit(solution)/shard_map/ppermute | solution.py:24
  111.3 72.2 %copy-start.1 = (f32[2,32,32]{2,1,0:T(8,128)S(1)}, f32[2,32,32]{2,1,0:T(8,128)}, u32[]{:S(2)}) copy-start(f32[2,32,32]{2,1,0:T(8,128)} %param.121) | copy-start | bytes 24580
  271.7 15.7 %collective-permute-start.14 = (f32[1,2,2,64]{3,2,1,0:T(2,128)S(1)}, f32[1,2,2,64]{3,2,1,0:T(2,128)S(1)}, u32[]{:S(2)}, u32[]{:S(2)}) collective-permute-start(f32[1,2,2,64]{3,2,1,0:T(2,128)S(1)} %maximum_bitcast_fusion.9), channel_id=1, source_target_pairs={{8,0},{16,8},{24,16},{9,1},{17,9},{25,17},{10,2},{18,10},{26,18},{... | collective-permute-start | bytes 3080 | tf_op jit(solution)/shard_map/ppermute | solution.py:24
  273.6 18.6 %collective-permute-start.13 = (f32[1,2,2,64]{3,2,1,0:T(2,128)S(1)}, f32[1,2,2,64]{3,2,1,0:T(2,128)S(1)}, u32[]{:S(2)}, u32[]{:S(2)}) collective-permute-start(f32[1,2,2,64]{3,2,1,0:T(2,128)S(1)} %maximum_bitcast_fusion.8), channel_id=1, source_target_pairs={{0,8},{8,16},{16,24},{1,9},{9,17},{17,25},{2,10},{10,18},{18,26},{... | collective-permute-start | bytes 3080 | tf_op jit(solution)/shard_map/ppermute | solution.py:23
  279.5 28.0 %collective-permute-start.19 = (f32[2,64,384]{2,1,0:T(8,128)}, f32[2,64,384]{2,1,0:T(8,128)S(1)}, u32[]{:S(2)}, u32[]{:S(2)}) collective-permute-start(f32[2,64,384]{2,1,0:T(8,128)} %get-tuple-element.737), channel_id=1, source_target_pairs={{2,0},{4,2},{6,4},{3,1},{5,3},{7,5},{10,8},{12,10},{14,12},{11,9},... | collective-permute-start | bytes 589832 | tf_op jit(solution)/shard_map/ppermute | solution.py:13
  283.2 21.9 %collective-permute-start.12 = (f32[2,64,384]{2,1,0:T(8,128)}, f32[2,64,384]{2,1,0:T(8,128)}, u32[]{:S(2)}, u32[]{:S(2)}) collective-permute-start(f32[2,64,384]{2,1,0:T(8,128)} %get-tuple-element.736), channel_id=1, source_target_pairs={{0,8},{8,16},{16,24},{1,9},{9,17},{17,25},{2,10},{10,18},{18,26},{... | collective-permute-start | bytes 589832 | tf_op jit(solution)/shard_map/ppermute | solution.py:13
  285.2 20.0 %collective-permute-start.18 = (f32[2,64,384]{2,1,0:T(8,128)}, f32[2,64,384]{2,1,0:T(8,128)S(1)}, u32[]{:S(2)}, u32[]{:S(2)}) collective-permute-start(f32[2,64,384]{2,1,0:T(8,128)} %get-tuple-element.739), channel_id=1, source_target_pairs={{0,2},{2,4},{4,6},{1,3},{3,5},{5,7},{8,10},{10,12},{12,14},{9,11},... | collective-permute-start | bytes 589832 | tf_op jit(solution)/shard_map/ppermute | solution.py:13
  287.4 21.5 %collective-permute-start.17 = (f32[2,64,384]{2,1,0:T(8,128)}, f32[2,64,384]{2,1,0:T(8,128)S(1)}, u32[]{:S(2)}, u32[]{:S(2)}) collective-permute-start(f32[2,64,384]{2,1,0:T(8,128)} %get-tuple-element.738), channel_id=1, source_target_pairs={{8,0},{16,8},{24,16},{9,1},{17,9},{25,17},{10,2},{18,10},{26,18},{... | collective-permute-start | bytes 589832 | tf_op jit(solution)/shard_map/ppermute | solution.py:13
  292.2 6.9 collective-permute-start.16
  299.1 5.8 collective-permute-start.15
  394.9 15.7 %collective-permute-start.22 = (f32[1,2,2,64]{3,2,1,0:T(2,128)S(1)}, f32[1,2,2,64]{3,2,1,0:T(2,128)S(1)}, u32[]{:S(2)}, u32[]{:S(2)}) collective-permute-start(f32[1,2,2,64]{3,2,1,0:T(2,128)S(1)} %maximum_bitcast_fusion.11), channel_id=1, source_target_pairs={{8,0},{16,8},{24,16},{9,1},{17,9},{25,17},{10,2},{18,10},{26,18},{... | collective-permute-start | bytes 3080 | tf_op jit(solution)/shard_map/ppermute | solution.py:24
  396.9 18.6 %collective-permute-start.21 = (f32[1,2,2,64]{3,2,1,0:T(2,128)S(1)}, f32[1,2,2,64]{3,2,1,0:T(2,128)S(1)}, u32[]{:S(2)}, u32[]{:S(2)}) collective-permute-start(f32[1,2,2,64]{3,2,1,0:T(2,128)S(1)} %maximum_bitcast_fusion.10), channel_id=1, source_target_pairs={{0,8},{8,16},{16,24},{1,9},{9,17},{17,25},{2,10},{10,18},{18,26},{... | collective-permute-start | bytes 3080 | tf_op jit(solution)/shard_map/ppermute | solution.py:23
  402.8 28.0 %collective-permute-start.27 = (f32[2,64,384]{2,1,0:T(8,128)}, f32[2,64,384]{2,1,0:T(8,128)S(1)}, u32[]{:S(2)}, u32[]{:S(2)}) collective-permute-start(f32[2,64,384]{2,1,0:T(8,128)} %get-tuple-element.733), channel_id=1, source_target_pairs={{2,0},{4,2},{6,4},{3,1},{5,3},{7,5},{10,8},{12,10},{14,12},{11,9},... | collective-permute-start | bytes 589832 | tf_op jit(solution)/shard_map/ppermute | solution.py:13
  404.8 23.7 %collective-permute-start.20 = (f32[2,64,384]{2,1,0:T(8,128)}, f32[2,64,384]{2,1,0:T(8,128)}, u32[]{:S(2)}, u32[]{:S(2)}) collective-permute-start(f32[2,64,384]{2,1,0:T(8,128)} %get-tuple-element.732), channel_id=1, source_target_pairs={{0,8},{8,16},{16,24},{1,9},{9,17},{17,25},{2,10},{10,18},{18,26},{... | collective-permute-start | bytes 589832 | tf_op jit(solution)/shard_map/ppermute | solution.py:13
  406.7 21.8 %collective-permute-start.26 = (f32[2,64,384]{2,1,0:T(8,128)}, f32[2,64,384]{2,1,0:T(8,128)S(1)}, u32[]{:S(2)}, u32[]{:S(2)}) collective-permute-start(f32[2,64,384]{2,1,0:T(8,128)} %get-tuple-element.735), channel_id=1, source_target_pairs={{0,2},{2,4},{4,6},{1,3},{3,5},{5,7},{8,10},{10,12},{12,14},{9,11},... | collective-permute-start | bytes 589832 | tf_op jit(solution)/shard_map/ppermute | solution.py:13
  410.6 21.5 %collective-permute-start.25 = (f32[2,64,384]{2,1,0:T(8,128)}, f32[2,64,384]{2,1,0:T(8,128)S(1)}, u32[]{:S(2)}, u32[]{:S(2)}) collective-permute-start(f32[2,64,384]{2,1,0:T(8,128)} %get-tuple-element.734), channel_id=1, source_target_pairs={{8,0},{16,8},{24,16},{9,1},{17,9},{25,17},{10,2},{18,10},{26,18},{... | collective-permute-start | bytes 589832 | tf_op jit(solution)/shard_map/ppermute | solution.py:13
  415.5 6.9 collective-permute-start.24
  422.4 5.8 collective-permute-start.23
  518.4 15.7 %collective-permute-start.30 = (f32[1,2,2,64]{3,2,1,0:T(2,128)S(1)}, f32[1,2,2,64]{3,2,1,0:T(2,128)S(1)}, u32[]{:S(2)}, u32[]{:S(2)}) collective-permute-start(f32[1,2,2,64]{3,2,1,0:T(2,128)S(1)} %maximum_bitcast_fusion.13), channel_id=1, source_target_pairs={{8,0},{16,8},{24,16},{9,1},{17,9},{25,17},{10,2},{18,10},{26,18},{... | collective-permute-start | bytes 3080 | tf_op jit(solution)/shard_map/ppermute | solution.py:24
  520.3 18.6 %collective-permute-start.29 = (f32[1,2,2,64]{3,2,1,0:T(2,128)S(1)}, f32[1,2,2,64]{3,2,1,0:T(2,128)S(1)}, u32[]{:S(2)}, u32[]{:S(2)}) collective-permute-start(f32[1,2,2,64]{3,2,1,0:T(2,128)S(1)} %maximum_bitcast_fusion.12), channel_id=1, source_target_pairs={{0,8},{8,16},{16,24},{1,9},{9,17},{17,25},{2,10},{10,18},{18,26},{... | collective-permute-start | bytes 3080 | tf_op jit(solution)/shard_map/ppermute | solution.py:23
  526.3 28.0 %collective-permute-start.35 = (f32[2,64,384]{2,1,0:T(8,128)}, f32[2,64,384]{2,1,0:T(8,128)S(1)}, u32[]{:S(2)}, u32[]{:S(2)}) collective-permute-start(f32[2,64,384]{2,1,0:T(8,128)} %get-tuple-element.729), channel_id=1, source_target_pairs={{2,0},{4,2},{6,4},{3,1},{5,3},{7,5},{10,8},{12,10},{14,12},{11,9},... | collective-permute-start | bytes 589832 | tf_op jit(solution)/shard_map/ppermute | solution.py:13
  528.2 23.7 %collective-permute-start.28 = (f32[2,64,384]{2,1,0:T(8,128)}, f32[2,64,384]{2,1,0:T(8,128)}, u32[]{:S(2)}, u32[]{:S(2)}) collective-permute-start(f32[2,64,384]{2,1,0:T(8,128)} %get-tuple-element.728), channel_id=1, source_target_pairs={{0,8},{8,16},{16,24},{1,9},{9,17},{17,25},{2,10},{10,18},{18,26},{... | collective-permute-start | bytes 589832 | tf_op jit(solution)/shard_map/ppermute | solution.py:13
  530.1 21.8 %collective-permute-start.34 = (f32[2,64,384]{2,1,0:T(8,128)}, f32[2,64,384]{2,1,0:T(8,128)S(1)}, u32[]{:S(2)}, u32[]{:S(2)}) collective-permute-start(f32[2,64,384]{2,1,0:T(8,128)} %get-tuple-element.731), channel_id=1, source_target_pairs={{0,2},{2,4},{4,6},{1,3},{3,5},{5,7},{8,10},{10,12},{12,14},{9,11},... | collective-permute-start | bytes 589832 | tf_op jit(solution)/shard_map/ppermute | solution.py:13
  534.1 21.5 %collective-permute-start.33 = (f32[2,64,384]{2,1,0:T(8,128)}, f32[2,64,384]{2,1,0:T(8,128)S(1)}, u32[]{:S(2)}, u32[]{:S(2)}) collective-permute-start(f32[2,64,384]{2,1,0:T(8,128)} %get-tuple-element.730), channel_id=1, source_target_pairs={{8,0},{16,8},{24,16},{9,1},{17,9},{25,17},{10,2},{18,10},{26,18},{... | collective-permute-start | bytes 589832 | tf_op jit(solution)/shard_map/ppermute | solution.py:13
  539.0 6.9 collective-permute-start.32
  545.8 5.8 collective-permute-start.31
  641.7 15.7 %collective-permute-start.38 = (f32[1,2,2,64]{3,2,1,0:T(2,128)S(1)}, f32[1,2,2,64]{3,2,1,0:T(2,128)S(1)}, u32[]{:S(2)}, u32[]{:S(2)}) collective-permute-start(f32[1,2,2,64]{3,2,1,0:T(2,128)S(1)} %maximum_bitcast_fusion.15), channel_id=1, source_target_pairs={{8,0},{16,8},{24,16},{9,1},{17,9},{25,17},{10,2},{18,10},{26,18},{... | collective-permute-start | bytes 3080 | tf_op jit(solution)/shard_map/ppermute | solution.py:24
  643.7 18.6 %collective-permute-start.37 = (f32[1,2,2,64]{3,2,1,0:T(2,128)S(1)}, f32[1,2,2,64]{3,2,1,0:T(2,128)S(1)}, u32[]{:S(2)}, u32[]{:S(2)}) collective-permute-start(f32[1,2,2,64]{3,2,1,0:T(2,128)S(1)} %maximum_bitcast_fusion.14), channel_id=1, source_target_pairs={{0,8},{8,16},{16,24},{1,9},{9,17},{17,25},{2,10},{10,18},{18,26},{... | collective-permute-start | bytes 3080 | tf_op jit(solution)/shard_map/ppermute | solution.py:23
  649.6 25.8 %collective-permute-start.43 = (f32[2,64,384]{2,1,0:T(8,128)S(1)}, f32[2,64,384]{2,1,0:T(8,128)S(1)}, u32[]{:S(2)}, u32[]{:S(2)}) collective-permute-start(f32[2,64,384]{2,1,0:T(8,128)S(1)} %get-tuple-element.725), channel_id=1, source_target_pairs={{2,0},{4,2},{6,4},{3,1},{5,3},{7,5},{10,8},{12,10},{14,12},{11,9},... | collective-permute-start | bytes 589832 | tf_op jit(solution)/shard_map/ppermute | solution.py:13
  651.5 23.7 %collective-permute-start.36 = (f32[2,64,384]{2,1,0:T(8,128)}, f32[2,64,384]{2,1,0:T(8,128)S(1)}, u32[]{:S(2)}, u32[]{:S(2)}) collective-permute-start(f32[2,64,384]{2,1,0:T(8,128)} %get-tuple-element.724), channel_id=1, source_target_pairs={{0,8},{8,16},{16,24},{1,9},{9,17},{17,25},{2,10},{10,18},{18,26},{... | collective-permute-start | bytes 589832 | tf_op jit(solution)/shard_map/ppermute | solution.py:13
  653.5 21.8 %collective-permute-start.42 = (f32[2,64,384]{2,1,0:T(8,128)}, f32[2,64,384]{2,1,0:T(8,128)S(1)}, u32[]{:S(2)}, u32[]{:S(2)}) collective-permute-start(f32[2,64,384]{2,1,0:T(8,128)} %get-tuple-element.727), channel_id=1, source_target_pairs={{0,2},{2,4},{4,6},{1,3},{3,5},{5,7},{8,10},{10,12},{12,14},{9,11},... | collective-permute-start | bytes 589832 | tf_op jit(solution)/shard_map/ppermute | solution.py:13
  657.4 18.5 %collective-permute-start.41 = (f32[2,64,384]{2,1,0:T(8,128)S(1)}, f32[2,64,384]{2,1,0:T(8,128)S(1)}, u32[]{:S(2)}, u32[]{:S(2)}) collective-permute-start(f32[2,64,384]{2,1,0:T(8,128)S(1)} %get-tuple-element.726), channel_id=1, source_target_pairs={{8,0},{16,8},{24,16},{9,1},{17,9},{25,17},{10,2},{18,10},{26,18},{... | collective-permute-start | bytes 589832 | tf_op jit(solution)/shard_map/ppermute | solution.py:13
  662.3 6.9 collective-permute-start.40
  669.1 5.8 collective-permute-start.39
  685.9 6.5 collective-permute-start.46
  687.8 6.4 collective-permute-start.45
  694.2 16.9 %collective-permute-start.48 = (f32[4,1,2,64]{3,2,1,0:T(2,128)S(1)}, f32[4,1,2,64]{3,2,1,0:T(2,128)S(1)}, u32[]{:S(2)}, u32[]{:S(2)}) collective-permute-start(f32[4,1,2,64]{3,2,1,0:T(2,128)S(1)} %get-tuple-element.813), channel_id=1, source_target_pairs={{2,0},{4,2},{6,4},{3,1},{5,3},{7,5},{10,8},{12,10},{14,12},{11,9},... | collective-permute-start | bytes 6152 | tf_op jit(solution)/shard_map/ppermute | solution.py:24
  698.4 18.7 %collective-permute-start.51 = (f32[2,64,384]{2,1,0:T(8,128)S(1)}, f32[2,64,384]{2,1,0:T(8,128)S(1)}, u32[]{:S(2)}, u32[]{:S(2)}) collective-permute-start(f32[2,64,384]{2,1,0:T(8,128)S(1)} %get-tuple-element.722), channel_id=1, source_target_pairs={{2,0},{4,2},{6,4},{3,1},{5,3},{7,5},{10,8},{12,10},{14,12},{11,9},... | collective-permute-start | bytes 589832 | tf_op jit(solution)/shard_map/ppermute | solution.py:13
  700.4 16.5 %collective-permute-start.44 = (f32[2,64,384]{2,1,0:T(8,128)S(1)}, f32[2,64,384]{2,1,0:T(8,128)S(1)}, u32[]{:S(2)}, u32[]{:S(2)}) collective-permute-start(f32[2,64,384]{2,1,0:T(8,128)S(1)} %get-tuple-element.720), channel_id=1, source_target_pairs={{0,8},{8,16},{16,24},{1,9},{9,17},{17,25},{2,10},{10,18},{18,26},{... | collective-permute-start | bytes 589832 | tf_op jit(solution)/shard_map/ppermute | solution.py:13
  703.4 13.5 %collective-permute-start.50 = (f32[2,64,384]{2,1,0:T(8,128)S(1)}, f32[2,64,384]{2,1,0:T(8,128)S(1)}, u32[]{:S(2)}, u32[]{:S(2)}) collective-permute-start(f32[2,64,384]{2,1,0:T(8,128)S(1)} %get-tuple-element.723), channel_id=1, source_target_pairs={{0,2},{2,4},{4,6},{1,3},{3,5},{5,7},{8,10},{10,12},{12,14},{9,11},... | collective-permute-start | bytes 589832 | tf_op jit(solution)/shard_map/ppermute | solution.py:13
  707.3 10.3 %collective-permute-start.49 = (f32[2,64,384]{2,1,0:T(8,128)S(1)}, f32[2,64,384]{2,1,0:T(8,128)S(1)}, u32[]{:S(2)}, u32[]{:S(2)}) collective-permute-start(f32[2,64,384]{2,1,0:T(8,128)S(1)} %get-tuple-element.721), channel_id=1, source_target_pairs={{8,0},{16,8},{24,16},{9,1},{17,9},{25,17},{10,2},{18,10},{26,18},{... | collective-permute-start | bytes 589832 | tf_op jit(solution)/shard_map/ppermute | solution.py:13
  711.1 5.5 collective-permute-start.47
where the time goes:
time: 732 us; the launch traced here: 721 us
  blocking collectives  355 us (48%)
  starting transfers between devices  163 us (22%)
  local copies, waits for them, and re-layouts  74.8 us (10%)
  matrix products  67.9 us (9%)
  waiting for transfers between devices  32.1 us (4%)
  other arithmetic  24.6 us (3%)
    psum x5, blocking collectives, per_device(): lax.psum(restrict_sum(outgoing, sender_weights), ('sy', 'sx'))  355 us
    ppermute x24, starting transfers between devices, shifted(): return lax.ppermute(value, axis, pairs)  75.5 us
    ppermute x14, starting transfers between devices, with_halo(): after = lax.ppermute(initial, axis, down)  50.4 us
    dot_general x6, matrix products, outgoing_traces(): jnp.dot(row_block, map_table, preferred_element_type=jnp.float32)  40.6 us
    ppermute x14, starting transfers between devices, with_halo(): before = lax.ppermute(last, axis, up)  37.3 us
    ppermute x14, waiting for transfers between devices, with_halo(): before = lax.ppermute(last, axis, up)  23 us
  transfers between devices with their start and end apart: 52, of which 13 were waited for; matrix products, arithmetic and copies ran while one was open for 7% of the time, Pallas kernels for 0%

commit v1 on v0

--- a/solution.py
+++ b/solution.py
@@ -163,7 +163,9 @@
         corrected = traces + spread.reshape(traces.shape)
         outgoing = outgoing_traces(corrected, interface_map, source_shard)
         if sweep_index + 1 < ITERS:
-            coarse_total = lax.psum(restrict_sum(outgoing, sender_weights), ("sy", "sx"))
+            coarse_total = jnp.sum(
+                lax.all_gather(restrict_sum(outgoing, sender_weights), ("sy", "sx")), axis=0
+            )
         traces = exchange_direct(outgoing)
     return (traces[None, None], coef_now)
 

time: 732 us -> 574 us (0.78)
  blocking collectives: 355 us -> 195 us
    psum x5 -> x0, blocking collectives: 355 us -> none  [per_device(): lax.psum(restrict_sum(outgoing, sender_weights), ('sy', 'sx'))]
    all_gather x0 -> x5, blocking collectives: none -> 195 us  [per_device(): lax.all_gather(restrict_sum(outgoing, sender_weights), ('sy', 'sx'))]
  transfers between devices with their start and end apart: 52 -> 52, of which waited for: 13 -> 13; matrix products, arithmetic and copies ran while one was open for 7% -> 9% of each run, Pallas kernels for 0% -> 0%
where the time goes in v1:
time: 574 us; the launch traced here: 563 us
  blocking collectives  195 us (34%)
  starting transfers between devices  165 us (29%)
  local copies, waits for them, and re-layouts  74.8 us (13%)
  matrix products  67.9 us (12%)
  waiting for transfers between devices  32.2 us (6%)
  other arithmetic  24.8 us (4%)
    all_gather x5, blocking collectives, per_device(): lax.all_gather(restrict_sum(outgoing, sender_weights), ('sy', 'sx'))  195 us
    ppermute x24, starting transfers between devices, shifted(): return lax.ppermute(value, axis, pairs)  82.2 us
    ppermute x14, starting transfers between devices, with_halo(): after = lax.ppermute(initial, axis, down)  50 us
    dot_general x6, matrix products, outgoing_traces(): jnp.dot(row_block, map_table, preferred_element_type=jnp.float32)  40.6 us
    ppermute x14, starting transfers between devices, with_halo(): before = lax.ppermute(last, axis, up)  32.5 us
    ppermute x14, waiting for transfers between devices, with_halo(): before = lax.ppermute(last, axis, up)  22.7 us
    scatter-add x12, local copies, waits for them, and re-layouts, assemble(): from_north.at[..., 0].add(0.5 * into_northwest).at[..., -1]  14.5 us
    dot_general x1, local copies, waits for them, and re-layouts, outgoing_traces(): jnp.dot(row_block, map_table, preferred_element_type=jnp.float32)  12.7 us
  transfers between devices with their start and end apart: 52, of which 13 were waited for; matrix products, arithmetic and copies ran while one was open for 9% of the time, Pallas kernels for 0%

profile of v1, /device:TPU:20, one launch (start us, length us, event | category | flops | bytes accessed | tf_op | source)
XLA Modules:
  0.0 563.0 jit_solution(6117901751935026167)
XLA Ops:
  2.5 9.8 %copy.404 = bf16[192,8,2,1536]{3,1,2,0:T(8,128)(2,1)} copy(bf16[192,8,2,1536]{3,2,1,0:T(2,128)(2,1)} %bitcast.756) | data formatting | bytes 18874368
  12.3 12.7 %copy.246 = bf16[3072,1536]{1,0:T(8,128)(2,1)} copy(bf16[3072,1536]{0,1:T(8,128)(2,1)} %bitcast.731) | data formatting | bytes 18874368 | tf_op jit(solution)/shard_map/dot_general | solution.py:82
  27.2 6.8 %fusion.29 = f32[2,64,2,1536]{3,1,2,0:T(8,128)S(1)} fusion(bf16[2,1536,1536,1]{2,1,0,3:T(8,128)(2,1)} %bitcast.725, bf16[1,64,1536]{2,1,0:T(8,128)(2,1)S(1)} %fusion.2, bf16[1,64,1536]{2,1,0:T(8,128)(2,1)S(1)} %fusion.3), kind=kOutput, calls=%fused_computation.106 | convolution fusion | flops 1208745984 | bytes 11403264 | tf_op jit(solution)/shard_map/dot_general | solution.py:82
  36.2 2.3 collective-permute-start.7
  38.8 3.4 collective-permute-start.2
  42.2 2.5 collective-permute-start.1
  44.7 1.9 collective-permute-start
  46.6 3.5 collective-permute-start.6
  51.9 4.8 collective-permute-start.5
  56.8 2.3 collective-permute-start.4
  60.1 2.2 collective-permute-done.4
  64.9 2.8 collective-permute-done.3
  71.3 4.8 collective-permute-start.9
  96.7 3.9 collective-permute-start.11
  102.5 5.2 collective-permute-done.11
  113.1 38.4 %all-gather = f32[32,64,32]{1,2,0:T(8,128)S(1)} all-gather(f32[2,64,32]{1,2,0:T(8,128)S(1)} %pad_maximum_fusion.1), channel_id=2, replica_groups=mesh['sy'=4,'sx'=4,'wl'=2] {'sy','sx'}, dimensions={0}, use_global_device_ids=true | all-gather | bytes 278528 | tf_op jit(solution)/shard_map/all_gather | solution.py:167
  156.6 6.8 %fusion.40 = f32[2,64,2,1536]{3,1,2,0:T(8,128)S(1)} fusion(bf16[2,1536,1536,1]{2,1,0,3:T(8,128)(2,1)} %bitcast.726, bf16[2,64,1536,1]{2,1,0,3:T(8,128)(2,1)S(1)} %reshape.2909), kind=kOutput, calls=%fused_computation.118 | convolution fusion | flops 1207959552 | bytes 11403264 | tf_op jit(solution)/shard_map/dot_general | solution.py:82
  166.9 42.0 %all-gather.1 = f32[32,64,32]{1,2,0:T(8,128)S(1)} all-gather(f32[2,64,32]{1,2,0:T(8,128)S(1)} %pad_maximum_fusion.2), channel_id=3, replica_groups=mesh['sy'=4,'sx'=4,'wl'=2] {'sy','sx'}, dimensions={0}, use_global_device_ids=true | all-gather | bytes 278528 | tf_op jit(solution)/shard_map/all_gather | solution.py:167
  209.4 3.0 collective-permute-start.14
  212.5 2.8 collective-permute-start.13
  217.3 5.8 %collective-permute-start.19 = (f32[2,64,384]{2,1,0:T(8,128)}, f32[2,64,384]{2,1,0:T(8,128)S(1)}, u32[]{:S(2)}, u32[]{:S(2)}) collective-permute-start(f32[2,64,384]{2,1,0:T(8,128)} %get-tuple-element.739), channel_id=1, source_target_pairs={{2,0},{4,2},{6,4},{3,1},{5,3},{7,5},{10,8},{12,10},{14,12},{11,9},... | collective-permute-start | bytes 589832 | tf_op jit(solution)/shard_map/ppermute | solution.py:13
  223.1 1.9 collective-permute-start.12
  225.1 1.9 collective-permute-start.18
  227.0 4.8 collective-permute-start.17
  231.9 4.0 collective-permute-start.16
  239.4 3.5 collective-permute-done.15
  251.8 6.8 %fusion.38 = f32[2,64,2,1536]{3,1,2,0:T(8,128)S(1)} fusion(bf16[2,1536,1536,1]{2,1,0,3:T(8,128)(2,1)} %bitcast.727, bf16[2,64,1536,1]{2,1,0,3:T(8,128)(2,1)S(1)} %reshape.2914), kind=kOutput, calls=%fused_computation.116 | convolution fusion | flops 1207959552 | bytes 11403264 | tf_op jit(solution)/shard_map/dot_general | solution.py:82
  262.0 38.5 %all-gather.2 = f32[32,64,32]{1,2,0:T(8,128)S(1)} all-gather(f32[2,64,32]{1,2,0:T(8,128)S(1)} %pad_maximum_fusion.3), channel_id=4, replica_groups=mesh['sy'=4,'sx'=4,'wl'=2] {'sy','sx'}, dimensions={0}, use_global_device_ids=true | all-gather | bytes 278528 | tf_op jit(solution)/shard_map/all_gather | solution.py:167
  301.0 3.4 collective-permute-start.22
  304.4 2.4 collective-permute-start.21
  308.9 5.7 %collective-permute-start.27 = (f32[2,64,384]{2,1,0:T(8,128)}, f32[2,64,384]{2,1,0:T(8,128)S(1)}, u32[]{:S(2)}, u32[]{:S(2)}) collective-permute-start(f32[2,64,384]{2,1,0:T(8,128)} %get-tuple-element.735), channel_id=1, source_target_pairs={{2,0},{4,2},{6,4},{3,1},{5,3},{7,5},{10,8},{12,10},{14,12},{11,9},... | collective-permute-start | bytes 589832 | tf_op jit(solution)/shard_map/ppermute | solution.py:13
  314.6 1.9 collective-permute-start.20
  316.6 1.9 collective-permute-start.26
  318.5 4.8 collective-permute-start.25
  323.4 4.1 collective-permute-start.24
  330.9 3.6 collective-permute-done.23
  340.0 2.1 scatter-add.229
  343.5 6.8 %fusion.36 = f32[2,64,2,1536]{3,1,2,0:T(8,128)S(1)} fusion(bf16[2,1536,1536,1]{2,1,0,3:T(8,128)(2,1)} %bitcast.728, bf16[2,64,1536,1]{2,1,0,3:T(8,128)(2,1)S(1)} %reshape.2919), kind=kOutput, calls=%fused_computation.114 | convolution fusion | flops 1207959552 | bytes 11403264 | tf_op jit(solution)/shard_map/dot_general | solution.py:82
  353.8 37.8 %all-gather.3 = f32[32,64,32]{1,2,0:T(8,128)S(1)} all-gather(f32[2,64,32]{1,2,0:T(8,128)S(1)} %pad_maximum_fusion.4), channel_id=5, replica_groups=mesh['sy'=4,'sx'=4,'wl'=2] {'sy','sx'}, dimensions={0}, use_global_device_ids=true | all-gather | bytes 278528 | tf_op jit(solution)/shard_map/all_gather | solution.py:167
  392.1 3.4 collective-permute-start.30
  395.5 2.5 collective-permute-start.29
  400.0 5.7 %collective-permute-start.35 = (f32[2,64,384]{2,1,0:T(8,128)}, f32[2,64,384]{2,1,0:T(8,128)S(1)}, u32[]{:S(2)}, u32[]{:S(2)}) collective-permute-start(f32[2,64,384]{2,1,0:T(8,128)} %get-tuple-element.731), channel_id=1, source_target_pairs={{2,0},{4,2},{6,4},{3,1},{5,3},{7,5},{10,8},{12,10},{14,12},{11,9},... | collective-permute-start | bytes 589832 | tf_op jit(solution)/shard_map/ppermute | solution.py:13
  405.7 1.9 collective-permute-start.28
  409.6 4.8 collective-permute-start.33
  414.4 4.1 collective-permute-start.32
  422.0 3.6 collective-permute-done.31
  434.4 6.8 %fusion.34 = f32[2,64,2,1536]{3,1,2,0:T(8,128)S(1)} fusion(bf16[2,1536,1536,1]{2,1,0,3:T(8,128)(2,1)} %bitcast.729, bf16[2,64,1536,1]{2,1,0,3:T(8,128)(2,1)S(1)} %reshape.2924), kind=kOutput, calls=%fused_computation.112 | convolution fusion | flops 1207959552 | bytes 11403264 | tf_op jit(solution)/shard_map/dot_general | solution.py:82
  444.5 38.2 %all-gather.4 = f32[32,64,32]{1,2,0:T(8,128)S(1)} all-gather(f32[2,64,32]{1,2,0:T(8,128)S(1)} %pad_maximum_fusion.5), channel_id=6, replica_groups=mesh['sy'=4,'sx'=4,'wl'=2] {'sy','sx'}, dimensions={0}, use_global_device_ids=true | all-gather | bytes 278528 | tf_op jit(solution)/shard_map/all_gather | solution.py:167
  483.2 2.6 collective-permute-start.38
  485.9 3.2 collective-permute-start.37
  491.1 4.9 collective-permute-start.43
  499.9 4.8 collective-permute-start.41
  504.8 5.0 collective-permute-start.40
  513.1 3.7 collective-permute-done.39
  520.2 6.8 %fusion.32 = f32[2,64,2,1536]{3,1,2,0:T(8,128)S(1)} fusion(bf16[2,1536,1536,1]{2,1,0,3:T(8,128)(2,1)} %bitcast.730, bf16[2,64,1536,1]{2,1,0,3:T(8,128)(2,1)S(1)} %reshape.2929), kind=kOutput, calls=%fused_computation.110 | convolution fusion | flops 1207959552 | bytes 11403264 | tf_op jit(solution)/shard_map/dot_general | solution.py:82
  527.8 2.0 collective-permute-start.46
  529.8 3.9 collective-permute-start.45
  536.2 3.9 collective-permute-start.48
  540.2 1.9 collective-permute-start.51
  542.1 3.2 collective-permute-start.44
  545.3 3.9 collective-permute-start.50
  549.3 3.7 collective-permute-start.49
  553.0 1.9 collective-permute-start.47
  555.1 3.5 collective-permute-done.47
  (395 shorter events, 125.4 us)
Async XLA Ops:
  12.3 12.7 %copy-start.2 = (f32[1,1,2,32,4,384]{5,4,3,2,1,0:T(4,128)S(1)}, f32[1,1,2,32,4,384]{5,4,3,2,1,0:T(4,128)}, u32[]{:S(2)}) copy-start(f32[1,1,2,32,4,384]{5,4,3,2,1,0:T(4,128)} %param.120) | copy-start | bytes 1179652
  34.1 1.1 copy-start
  35.3 14.8 %copy-start.3 = (f32[1,1,2,32,4,384]{5,4,3,2,1,0:T(4,128)S(1)}, f32[1,1,2,32,4,384]{5,4,3,2,1,0:T(4,128)}, u32[]{:S(2)}) copy-start(f32[1,1,2,32,4,384]{5,4,3,2,1,0:T(4,128)} %param.119) | copy-start | bytes 1179652
  36.2 43.0 %collective-permute-start.7 = (f32[2,64,384]{2,1,0:T(8,128)}, f32[2,64,384]{2,1,0:T(8,128)S(1)}, u32[]{:S(2)}, u32[]{:S(2)}) collective-permute-start(f32[2,64,384]{2,1,0:T(8,128)} %get-tuple-element.743), channel_id=1, source_target_pairs={{2,0},{4,2},{6,4},{3,1},{5,3},{7,5},{10,8},{12,10},{14,12},{11,9},... | collective-permute-start | bytes 589832 | tf_op jit(solution)/shard_map/ppermute | solution.py:13
  38.8 13.1 %collective-permute-start.2 = (f32[1,2,2,64]{3,2,1,0:T(2,128)S(1)}, f32[1,2,2,64]{3,2,1,0:T(2,128)S(1)}, u32[]{:S(2)}, u32[]{:S(2)}) collective-permute-start(f32[1,2,2,64]{3,2,1,0:T(2,128)S(1)} %maximum_bitcast_fusion.7), channel_id=1, source_target_pairs={{8,0},{16,8},{24,16},{9,1},{17,9},{25,17},{10,2},{18,10},{26,18},{... | collective-permute-start | bytes 3080 | tf_op jit(solution)/shard_map/ppermute | solution.py:24
  42.2 14.5 %collective-permute-start.1 = (f32[1,2,2,64]{3,2,1,0:T(2,128)S(1)}, f32[1,2,2,64]{3,2,1,0:T(2,128)S(1)}, u32[]{:S(2)}, u32[]{:S(2)}) collective-permute-start(f32[1,2,2,64]{3,2,1,0:T(2,128)S(1)} %maximum_bitcast_fusion.6), channel_id=1, source_target_pairs={{0,8},{8,16},{16,24},{1,9},{9,17},{17,25},{2,10},{10,18},{18,26},{... | collective-permute-start | bytes 3080 | tf_op jit(solution)/shard_map/ppermute | solution.py:23
  44.7 26.6 %collective-permute-start = (f32[2,64,384]{2,1,0:T(8,128)S(1)}, f32[2,64,384]{2,1,0:T(8,128)}, u32[]{:S(2)}, u32[]{:S(2)}) collective-permute-start(f32[2,64,384]{2,1,0:T(8,128)S(1)} %get-tuple-element.742), channel_id=1, source_target_pairs={{0,8},{8,16},{16,24},{1,9},{9,17},{17,25},{2,10},{10,18},{18,26},{... | collective-permute-start | bytes 589832 | tf_op jit(solution)/shard_map/ppermute | solution.py:13
  46.6 29.5 %collective-permute-start.6 = (f32[2,64,384]{2,1,0:T(8,128)}, f32[2,64,384]{2,1,0:T(8,128)}, u32[]{:S(2)}, u32[]{:S(2)}) collective-permute-start(f32[2,64,384]{2,1,0:T(8,128)} %get-tuple-element.745), channel_id=1, source_target_pairs={{0,2},{2,4},{4,6},{1,3},{3,5},{5,7},{8,10},{10,12},{12,14},{9,11},... | collective-permute-start | bytes 589832 | tf_op jit(solution)/shard_map/ppermute | solution.py:13
  51.9 31.4 %collective-permute-start.5 = (f32[2,64,384]{2,1,0:T(8,128)}, f32[2,64,384]{2,1,0:T(8,128)}, u32[]{:S(2)}, u32[]{:S(2)}) collective-permute-start(f32[2,64,384]{2,1,0:T(8,128)} %get-tuple-element.744), channel_id=1, source_target_pairs={{8,0},{16,8},{24,16},{9,1},{17,9},{25,17},{10,2},{18,10},{26,18},{... | collective-permute-start | bytes 589832 | tf_op jit(solution)/shard_map/ppermute | solution.py:13
  56.8 5.5 collective-permute-start.4
  62.3 5.5 collective-permute-start.3
  67.8 18.6 %collective-permute-start.8 = (f32[1,3,2,32,384]{4,3,2,1,0:T(8,128)}, f32[1,3,2,32,384]{4,3,2,1,0:T(8,128)S(1)}, u32[]{:S(2)}, u32[]{:S(2)}) collective-permute-start(f32[1,3,2,32,384]{4,3,2,1,0:T(8,128)} %maximum_bitcast_fusion.3), channel_id=1, source_target_pairs={{0,8},{8,16},{16,24},{1,9},{9,17},{17,25},{2,10},{10,18},{18,26},{... | collective-permute-start | bytes 884744 | tf_op jit(solution)/shard_map/ppermute | solution.py:23
  71.3 16.2 %collective-permute-start.9 = (f32[1,3,2,32,384]{4,3,2,1,0:T(8,128)}, f32[1,3,2,32,384]{4,3,2,1,0:T(8,128)S(1)}, u32[]{:S(2)}, u32[]{:S(2)}) collective-permute-start(f32[1,3,2,32,384]{4,3,2,1,0:T(8,128)} %maximum_bitcast_fusion.4), channel_id=1, source_target_pairs={{8,0},{16,8},{24,16},{9,1},{17,9},{25,17},{10,2},{18,10},{26,18},{... | collective-permute-start | bytes 884744 | tf_op jit(solution)/shard_map/ppermute | solution.py:24
  87.5 4.3 copy-start.5
  87.5 7.6 %copy-start.4 = (f32[2,64,1,1]{3,1,0,2:T(8,128)S(1)}, f32[2,64,1,1]{3,1,0,2:T(8,128)}, u32[]{:S(2)}) copy-start(f32[2,64,1,1]{3,1,0,2:T(8,128)} %get-tuple-element.806) | copy-start | bytes 1540
  88.5 12.1 %collective-permute-start.10 = (f32[5,1,2,32,384]{4,3,2,1,0:T(8,128)}, f32[5,1,2,32,384]{4,3,2,1,0:T(8,128)}, u32[]{:S(2)}, u32[]{:S(2)}) collective-permute-start(f32[5,1,2,32,384]{4,3,2,1,0:T(8,128)} %get-tuple-element.720), channel_id=1, source_target_pairs={{0,2},{2,4},{4,6},{1,3},{3,5},{5,7},{8,10},{10,12},{12,14},{9,11},... | collective-permute-start | bytes 1474568 | tf_op jit(solution)/shard_map/ppermute | solution.py:23
  96.7 11.0 %collective-permute-start.11 = (f32[5,1,2,32,384]{4,3,2,1,0:T(8,128)}, f32[5,1,2,32,384]{4,3,2,1,0:T(8,128)}, u32[]{:S(2)}, u32[]{:S(2)}) collective-permute-start(f32[5,1,2,32,384]{4,3,2,1,0:T(8,128)} %get-tuple-element.721), channel_id=1, source_target_pairs={{2,0},{4,2},{6,4},{3,1},{5,3},{7,5},{10,8},{12,10},{14,12},{11,9},... | collective-permute-start | bytes 1474568 | tf_op jit(solution)/shard_map/ppermute | solution.py:24
  111.8 39.8 %copy-start.1 = (f32[2,32,32]{2,1,0:T(8,128)S(1)}, f32[2,32,32]{2,1,0:T(8,128)}, u32[]{:S(2)}) copy-start(f32[2,32,32]{2,1,0:T(8,128)} %param.121) | copy-start | bytes 24580
  209.4 17.6 %collective-permute-start.14 = (f32[1,2,2,64]{3,2,1,0:T(2,128)S(1)}, f32[1,2,2,64]{3,2,1,0:T(2,128)S(1)}, u32[]{:S(2)}, u32[]{:S(2)}) collective-permute-start(f32[1,2,2,64]{3,2,1,0:T(2,128)S(1)} %maximum_bitcast_fusion.9), channel_id=1, source_target_pairs={{8,0},{16,8},{24,16},{9,1},{17,9},{25,17},{10,2},{18,10},{26,18},{... | collective-permute-start | bytes 3080 | tf_op jit(solution)/shard_map/ppermute | solution.py:24
  212.5 19.3 %collective-permute-start.13 = (f32[1,2,2,64]{3,2,1,0:T(2,128)S(1)}, f32[1,2,2,64]{3,2,1,0:T(2,128)S(1)}, u32[]{:S(2)}, u32[]{:S(2)}) collective-permute-start(f32[1,2,2,64]{3,2,1,0:T(2,128)S(1)} %maximum_bitcast_fusion.8), channel_id=1, source_target_pairs={{0,8},{8,16},{16,24},{1,9},{9,17},{17,25},{2,10},{10,18},{18,26},{... | collective-permute-start | bytes 3080 | tf_op jit(solution)/shard_map/ppermute | solution.py:23
  217.3 28.4 %collective-permute-start.19 = (f32[2,64,384]{2,1,0:T(8,128)}, f32[2,64,384]{2,1,0:T(8,128)S(1)}, u32[]{:S(2)}, u32[]{:S(2)}) collective-permute-start(f32[2,64,384]{2,1,0:T(8,128)} %get-tuple-element.739), channel_id=1, source_target_pairs={{2,0},{4,2},{6,4},{3,1},{5,3},{7,5},{10,8},{12,10},{14,12},{11,9},... | collective-permute-start | bytes 589832 | tf_op jit(solution)/shard_map/ppermute | solution.py:13
  223.1 20.2 %collective-permute-start.12 = (f32[2,64,384]{2,1,0:T(8,128)}, f32[2,64,384]{2,1,0:T(8,128)}, u32[]{:S(2)}, u32[]{:S(2)}) collective-permute-start(f32[2,64,384]{2,1,0:T(8,128)} %get-tuple-element.738), channel_id=1, source_target_pairs={{0,8},{8,16},{16,24},{1,9},{9,17},{17,25},{2,10},{10,18},{18,26},{... | collective-permute-start | bytes 589832 | tf_op jit(solution)/shard_map/ppermute | solution.py:13
  225.1 18.2 %collective-permute-start.18 = (f32[2,64,384]{2,1,0:T(8,128)}, f32[2,64,384]{2,1,0:T(8,128)S(1)}, u32[]{:S(2)}, u32[]{:S(2)}) collective-permute-start(f32[2,64,384]{2,1,0:T(8,128)} %get-tuple-element.741), channel_id=1, source_target_pairs={{0,2},{2,4},{4,6},{1,3},{3,5},{5,7},{8,10},{10,12},{12,14},{9,11},... | collective-permute-start | bytes 589832 | tf_op jit(solution)/shard_map/ppermute | solution.py:13
  227.0 20.0 %collective-permute-start.17 = (f32[2,64,384]{2,1,0:T(8,128)}, f32[2,64,384]{2,1,0:T(8,128)S(1)}, u32[]{:S(2)}, u32[]{:S(2)}) collective-permute-start(f32[2,64,384]{2,1,0:T(8,128)} %get-tuple-element.740), channel_id=1, source_target_pairs={{8,0},{16,8},{24,16},{9,1},{17,9},{25,17},{10,2},{18,10},{26,18},{... | collective-permute-start | bytes 589832 | tf_op jit(solution)/shard_map/ppermute | solution.py:13
  231.9 5.5 collective-permute-start.16
  237.4 5.6 collective-permute-start.15
  301.0 17.5 %collective-permute-start.22 = (f32[1,2,2,64]{3,2,1,0:T(2,128)S(1)}, f32[1,2,2,64]{3,2,1,0:T(2,128)S(1)}, u32[]{:S(2)}, u32[]{:S(2)}) collective-permute-start(f32[1,2,2,64]{3,2,1,0:T(2,128)S(1)} %maximum_bitcast_fusion.11), channel_id=1, source_target_pairs={{8,0},{16,8},{24,16},{9,1},{17,9},{25,17},{10,2},{18,10},{26,18},{... | collective-permute-start | bytes 3080 | tf_op jit(solution)/shard_map/ppermute | solution.py:24
  304.4 18.9 %collective-permute-start.21 = (f32[1,2,2,64]{3,2,1,0:T(2,128)S(1)}, f32[1,2,2,64]{3,2,1,0:T(2,128)S(1)}, u32[]{:S(2)}, u32[]{:S(2)}) collective-permute-start(f32[1,2,2,64]{3,2,1,0:T(2,128)S(1)} %maximum_bitcast_fusion.10), channel_id=1, source_target_pairs={{0,8},{8,16},{16,24},{1,9},{9,17},{17,25},{2,10},{10,18},{18,26},{... | collective-permute-start | bytes 3080 | tf_op jit(solution)/shard_map/ppermute | solution.py:23
  308.9 28.4 %collective-permute-start.27 = (f32[2,64,384]{2,1,0:T(8,128)}, f32[2,64,384]{2,1,0:T(8,128)S(1)}, u32[]{:S(2)}, u32[]{:S(2)}) collective-permute-start(f32[2,64,384]{2,1,0:T(8,128)} %get-tuple-element.735), channel_id=1, source_target_pairs={{2,0},{4,2},{6,4},{3,1},{5,3},{7,5},{10,8},{12,10},{14,12},{11,9},... | collective-permute-start | bytes 589832 | tf_op jit(solution)/shard_map/ppermute | solution.py:13
  314.6 20.3 %collective-permute-start.20 = (f32[2,64,384]{2,1,0:T(8,128)}, f32[2,64,384]{2,1,0:T(8,128)}, u32[]{:S(2)}, u32[]{:S(2)}) collective-permute-start(f32[2,64,384]{2,1,0:T(8,128)} %get-tuple-element.734), channel_id=1, source_target_pairs={{0,8},{8,16},{16,24},{1,9},{9,17},{17,25},{2,10},{10,18},{18,26},{... | collective-permute-start | bytes 589832 | tf_op jit(solution)/shard_map/ppermute | solution.py:13
  316.6 18.3 %collective-permute-start.26 = (f32[2,64,384]{2,1,0:T(8,128)}, f32[2,64,384]{2,1,0:T(8,128)S(1)}, u32[]{:S(2)}, u32[]{:S(2)}) collective-permute-start(f32[2,64,384]{2,1,0:T(8,128)} %get-tuple-element.737), channel_id=1, source_target_pairs={{0,2},{2,4},{4,6},{1,3},{3,5},{5,7},{8,10},{10,12},{12,14},{9,11},... | collective-permute-start | bytes 589832 | tf_op jit(solution)/shard_map/ppermute | solution.py:13
  318.5 20.1 %collective-permute-start.25 = (f32[2,64,384]{2,1,0:T(8,128)}, f32[2,64,384]{2,1,0:T(8,128)S(1)}, u32[]{:S(2)}, u32[]{:S(2)}) collective-permute-start(f32[2,64,384]{2,1,0:T(8,128)} %get-tuple-element.736), channel_id=1, source_target_pairs={{8,0},{16,8},{24,16},{9,1},{17,9},{25,17},{10,2},{18,10},{26,18},{... | collective-permute-start | bytes 589832 | tf_op jit(solution)/shard_map/ppermute | solution.py:13
  323.4 5.5 collective-permute-start.24
  328.9 5.7 %collective-permute-start.23 = (f32[4,1,2,64]{3,2,1,0:T(2,128)S(1)}, f32[4,1,2,64]{3,2,1,0:T(2,128)S(1)}, u32[]{:S(2)}, u32[]{:S(2)}) collective-permute-start(f32[4,1,2,64]{3,2,1,0:T(2,128)S(1)} %get-tuple-element.820), channel_id=1, source_target_pairs={{0,2},{2,4},{4,6},{1,3},{3,5},{5,7},{8,10},{10,12},{12,14},{9,11},... | collective-permute-start | bytes 6152 | tf_op jit(solution)/shard_map/ppermute | solution.py:23
  392.1 17.4 %collective-permute-start.30 = (f32[1,2,2,64]{3,2,1,0:T(2,128)S(1)}, f32[1,2,2,64]{3,2,1,0:T(2,128)S(1)}, u32[]{:S(2)}, u32[]{:S(2)}) collective-permute-start(f32[1,2,2,64]{3,2,1,0:T(2,128)S(1)} %maximum_bitcast_fusion.13), channel_id=1, source_target_pairs={{8,0},{16,8},{24,16},{9,1},{17,9},{25,17},{10,2},{18,10},{26,18},{... | collective-permute-start | bytes 3080 | tf_op jit(solution)/shard_map/ppermute | solution.py:24
  395.5 18.9 %collective-permute-start.29 = (f32[1,2,2,64]{3,2,1,0:T(2,128)S(1)}, f32[1,2,2,64]{3,2,1,0:T(2,128)S(1)}, u32[]{:S(2)}, u32[]{:S(2)}) collective-permute-start(f32[1,2,2,64]{3,2,1,0:T(2,128)S(1)} %maximum_bitcast_fusion.12), channel_id=1, source_target_pairs={{0,8},{8,16},{16,24},{1,9},{9,17},{17,25},{2,10},{10,18},{18,26},{... | collective-permute-start | bytes 3080 | tf_op jit(solution)/shard_map/ppermute | solution.py:23
  400.0 28.3 %collective-permute-start.35 = (f32[2,64,384]{2,1,0:T(8,128)}, f32[2,64,384]{2,1,0:T(8,128)S(1)}, u32[]{:S(2)}, u32[]{:S(2)}) collective-permute-start(f32[2,64,384]{2,1,0:T(8,128)} %get-tuple-element.731), channel_id=1, source_target_pairs={{2,0},{4,2},{6,4},{3,1},{5,3},{7,5},{10,8},{12,10},{14,12},{11,9},... | collective-permute-start | bytes 589832 | tf_op jit(solution)/shard_map/ppermute | solution.py:13
  405.7 20.2 %collective-permute-start.28 = (f32[2,64,384]{2,1,0:T(8,128)}, f32[2,64,384]{2,1,0:T(8,128)}, u32[]{:S(2)}, u32[]{:S(2)}) collective-permute-start(f32[2,64,384]{2,1,0:T(8,128)} %get-tuple-element.730), channel_id=1, source_target_pairs={{0,8},{8,16},{16,24},{1,9},{9,17},{17,25},{2,10},{10,18},{18,26},{... | collective-permute-start | bytes 589832 | tf_op jit(solution)/shard_map/ppermute | solution.py:13
  407.6 18.3 %collective-permute-start.34 = (f32[2,64,384]{2,1,0:T(8,128)}, f32[2,64,384]{2,1,0:T(8,128)S(1)}, u32[]{:S(2)}, u32[]{:S(2)}) collective-permute-start(f32[2,64,384]{2,1,0:T(8,128)} %get-tuple-element.733), channel_id=1, source_target_pairs={{0,2},{2,4},{4,6},{1,3},{3,5},{5,7},{8,10},{10,12},{12,14},{9,11},... | collective-permute-start | bytes 589832 | tf_op jit(solution)/shard_map/ppermute | solution.py:13
  409.6 20.1 %collective-permute-start.33 = (f32[2,64,384]{2,1,0:T(8,128)}, f32[2,64,384]{2,1,0:T(8,128)S(1)}, u32[]{:S(2)}, u32[]{:S(2)}) collective-permute-start(f32[2,64,384]{2,1,0:T(8,128)} %get-tuple-element.732), channel_id=1, source_target_pairs={{8,0},{16,8},{24,16},{9,1},{17,9},{25,17},{10,2},{18,10},{26,18},{... | collective-permute-start | bytes 589832 | tf_op jit(solution)/shard_map/ppermute | solution.py:13
  414.4 5.5 collective-permute-start.32
  419.9 5.7 %collective-permute-start.31 = (f32[4,1,2,64]{3,2,1,0:T(2,128)S(1)}, f32[4,1,2,64]{3,2,1,0:T(2,128)S(1)}, u32[]{:S(2)}, u32[]{:S(2)}) collective-permute-start(f32[4,1,2,64]{3,2,1,0:T(2,128)S(1)} %get-tuple-element.818), channel_id=1, source_target_pairs={{0,2},{2,4},{4,6},{1,3},{3,5},{5,7},{8,10},{10,12},{12,14},{9,11},... | collective-permute-start | bytes 6152 | tf_op jit(solution)/shard_map/ppermute | solution.py:23
  483.2 16.7 %collective-permute-start.38 = (f32[1,2,2,64]{3,2,1,0:T(2,128)S(1)}, f32[1,2,2,64]{3,2,1,0:T(2,128)S(1)}, u32[]{:S(2)}, u32[]{:S(2)}) collective-permute-start(f32[1,2,2,64]{3,2,1,0:T(2,128)S(1)} %maximum_bitcast_fusion.15), channel_id=1, source_target_pairs={{8,0},{16,8},{24,16},{9,1},{17,9},{25,17},{10,2},{18,10},{26,18},{... | collective-permute-start | bytes 3080 | tf_op jit(solution)/shard_map/ppermute | solution.py:24
  485.9 18.9 %collective-permute-start.37 = (f32[1,2,2,64]{3,2,1,0:T(2,128)S(1)}, f32[1,2,2,64]{3,2,1,0:T(2,128)S(1)}, u32[]{:S(2)}, u32[]{:S(2)}) collective-permute-start(f32[1,2,2,64]{3,2,1,0:T(2,128)S(1)} %maximum_bitcast_fusion.14), channel_id=1, source_target_pairs={{0,8},{8,16},{16,24},{1,9},{9,17},{17,25},{2,10},{10,18},{18,26},{... | collective-permute-start | bytes 3080 | tf_op jit(solution)/shard_map/ppermute | solution.py:23
  491.1 26.3 %collective-permute-start.43 = (f32[2,64,384]{2,1,0:T(8,128)S(1)}, f32[2,64,384]{2,1,0:T(8,128)S(1)}, u32[]{:S(2)}, u32[]{:S(2)}) collective-permute-start(f32[2,64,384]{2,1,0:T(8,128)S(1)} %get-tuple-element.727), channel_id=1, source_target_pairs={{2,0},{4,2},{6,4},{3,1},{5,3},{7,5},{10,8},{12,10},{14,12},{11,9},... | collective-permute-start | bytes 589832 | tf_op jit(solution)/shard_map/ppermute | solution.py:13
  496.0 21.2 %collective-permute-start.36 = (f32[2,64,384]{2,1,0:T(8,128)}, f32[2,64,384]{2,1,0:T(8,128)S(1)}, u32[]{:S(2)}, u32[]{:S(2)}) collective-permute-start(f32[2,64,384]{2,1,0:T(8,128)} %get-tuple-element.726), channel_id=1, source_target_pairs={{0,8},{8,16},{16,24},{1,9},{9,17},{17,25},{2,10},{10,18},{18,26},{... | collective-permute-start | bytes 589832 | tf_op jit(solution)/shard_map/ppermute | solution.py:13
  498.0 19.2 %collective-permute-start.42 = (f32[2,64,384]{2,1,0:T(8,128)}, f32[2,64,384]{2,1,0:T(8,128)S(1)}, u32[]{:S(2)}, u32[]{:S(2)}) collective-permute-start(f32[2,64,384]{2,1,0:T(8,128)} %get-tuple-element.729), channel_id=1, source_target_pairs={{0,2},{2,4},{4,6},{1,3},{3,5},{5,7},{8,10},{10,12},{12,14},{9,11},... | collective-permute-start | bytes 589832 | tf_op jit(solution)/shard_map/ppermute | solution.py:13
  499.9 18.0 %collective-permute-start.41 = (f32[2,64,384]{2,1,0:T(8,128)S(1)}, f32[2,64,384]{2,1,0:T(8,128)S(1)}, u32[]{:S(2)}, u32[]{:S(2)}) collective-permute-start(f32[2,64,384]{2,1,0:T(8,128)S(1)} %get-tuple-element.728), channel_id=1, source_target_pairs={{8,0},{16,8},{24,16},{9,1},{17,9},{25,17},{10,2},{18,10},{26,18},{... | collective-permute-start | bytes 589832 | tf_op jit(solution)/shard_map/ppermute | solution.py:13
  504.8 6.3 %collective-permute-start.40 = (f32[4,1,2,64]{3,2,1,0:T(2,128)S(1)}, f32[4,1,2,64]{3,2,1,0:T(2,128)S(1)}, u32[]{:S(2)}, u32[]{:S(2)}) collective-permute-start(f32[4,1,2,64]{3,2,1,0:T(2,128)S(1)} %get-tuple-element.817), channel_id=1, source_target_pairs={{2,0},{4,2},{6,4},{3,1},{5,3},{7,5},{10,8},{12,10},{14,12},{11,9},... | collective-permute-start | bytes 6152 | tf_op jit(solution)/shard_map/ppermute | solution.py:24
  511.1 5.8 %collective-permute-start.39 = (f32[4,1,2,64]{3,2,1,0:T(2,128)S(1)}, f32[4,1,2,64]{3,2,1,0:T(2,128)S(1)}, u32[]{:S(2)}, u32[]{:S(2)}) collective-permute-start(f32[4,1,2,64]{3,2,1,0:T(2,128)S(1)} %get-tuple-element.816), channel_id=1, source_target_pairs={{0,2},{2,4},{4,6},{1,3},{3,5},{5,7},{8,10},{10,12},{12,14},{9,11},... | collective-permute-start | bytes 6152 | tf_op jit(solution)/shard_map/ppermute | solution.py:23
  527.8 6.5 %collective-permute-start.46 = (f32[1,2,2,64]{3,2,1,0:T(2,128)S(1)}, f32[1,2,2,64]{3,2,1,0:T(2,128)S(1)}, u32[]{:S(2)}, u32[]{:S(2)}) collective-permute-start(f32[1,2,2,64]{3,2,1,0:T(2,128)S(1)} %maximum_bitcast_fusion.17), channel_id=1, source_target_pairs={{8,0},{16,8},{24,16},{9,1},{17,9},{25,17},{10,2},{18,10},{26,18},{... | collective-permute-start | bytes 3080 | tf_op jit(solution)/shard_map/ppermute | solution.py:24
  529.8 6.4 %collective-permute-start.45 = (f32[1,2,2,64]{3,2,1,0:T(2,128)S(1)}, f32[1,2,2,64]{3,2,1,0:T(2,128)S(1)}, u32[]{:S(2)}, u32[]{:S(2)}) collective-permute-start(f32[1,2,2,64]{3,2,1,0:T(2,128)S(1)} %maximum_bitcast_fusion.16), channel_id=1, source_target_pairs={{0,8},{8,16},{16,24},{1,9},{9,17},{17,25},{2,10},{10,18},{18,26},{... | collective-permute-start | bytes 3080 | tf_op jit(solution)/shard_map/ppermute | solution.py:23
  536.2 16.8 %collective-permute-start.48 = (f32[4,1,2,64]{3,2,1,0:T(2,128)S(1)}, f32[4,1,2,64]{3,2,1,0:T(2,128)S(1)}, u32[]{:S(2)}, u32[]{:S(2)}) collective-permute-start(f32[4,1,2,64]{3,2,1,0:T(2,128)S(1)} %get-tuple-element.815), channel_id=1, source_target_pairs={{2,0},{4,2},{6,4},{3,1},{5,3},{7,5},{10,8},{12,10},{14,12},{11,9},... | collective-permute-start | bytes 6152 | tf_op jit(solution)/shard_map/ppermute | solution.py:24
  540.2 18.9 %collective-permute-start.51 = (f32[2,64,384]{2,1,0:T(8,128)S(1)}, f32[2,64,384]{2,1,0:T(8,128)S(1)}, u32[]{:S(2)}, u32[]{:S(2)}) collective-permute-start(f32[2,64,384]{2,1,0:T(8,128)S(1)} %get-tuple-element.724), channel_id=1, source_target_pairs={{2,0},{4,2},{6,4},{3,1},{5,3},{7,5},{10,8},{12,10},{14,12},{11,9},... | collective-permute-start | bytes 589832 | tf_op jit(solution)/shard_map/ppermute | solution.py:13
  542.1 16.8 %collective-permute-start.44 = (f32[2,64,384]{2,1,0:T(8,128)S(1)}, f32[2,64,384]{2,1,0:T(8,128)S(1)}, u32[]{:S(2)}, u32[]{:S(2)}) collective-permute-start(f32[2,64,384]{2,1,0:T(8,128)S(1)} %get-tuple-element.722), channel_id=1, source_target_pairs={{0,8},{8,16},{16,24},{1,9},{9,17},{17,25},{2,10},{10,18},{18,26},{... | collective-permute-start | bytes 589832 | tf_op jit(solution)/shard_map/ppermute | solution.py:13
  545.3 13.5 %collective-permute-start.50 = (f32[2,64,384]{2,1,0:T(8,128)S(1)}, f32[2,64,384]{2,1,0:T(8,128)S(1)}, u32[]{:S(2)}, u32[]{:S(2)}) collective-permute-start(f32[2,64,384]{2,1,0:T(8,128)S(1)} %get-tuple-element.725), channel_id=1, source_target_pairs={{0,2},{2,4},{4,6},{1,3},{3,5},{5,7},{8,10},{10,12},{12,14},{9,11},... | collective-permute-start | bytes 589832 | tf_op jit(solution)/shard_map/ppermute | solution.py:13
  549.3 10.3 %collective-permute-start.49 = (f32[2,64,384]{2,1,0:T(8,128)S(1)}, f32[2,64,384]{2,1,0:T(8,128)S(1)}, u32[]{:S(2)}, u32[]{:S(2)}) collective-permute-start(f32[2,64,384]{2,1,0:T(8,128)S(1)} %get-tuple-element.723), channel_id=1, source_target_pairs={{8,0},{16,8},{24,16},{9,1},{17,9},{25,17},{10,2},{18,10},{26,18},{... | collective-permute-start | bytes 589832 | tf_op jit(solution)/shard_map/ppermute | solution.py:13
  553.0 5.5 collective-permute-start.47
